TPU v7x, 32 devices: a whole 2x2x4 slice. The times are simulated.
32 devices in a mesh: rows: 8 (over z, y), cols: 4 (over x, core).
Axes of the slice: x: 2, y: 2, z: 4, core: 2. Of those that a mesh axis runs over, the one named last changes fastest.
Arguments:
- features: bfloat16 [64, 512, 512], P('rows', 'cols'), may hold values from -6 to 6
- dw_weight: float32 [49, 512], replicated, may hold values from -0.875 to 0.875
- norm_gain: float32 [512], replicated, may hold values from 0.1 to 1.9
- w_up: bfloat16 [512, 2048], replicated, may hold values from -0.25 to 0.25
- w_down: bfloat16 [2048, 512], replicated, may hold values from -0.125 to 0.125
- cotangent: bfloat16 [64, 512, 512], P('rows', 'cols'), may hold values from -6 to 6
Outputs:
- grad_input: bfloat16 [64, 512, 512], P('rows', 'cols')
- grad_dw: float32 [49, 512], replicated
- grad_gain: float32 [512], replicated
- grad_up: float32 [512, 2048], replicated
- grad_down: float32 [2048, 512], replicated
All inputs are finite; a program needn't handle non-finite values.
Results may differ from a plain program's by a relative error of at most 0.019.
Values may be sent and summed in bfloat16 or wider, within the bound.
A program may use at most 128 MiB of HBM per device.

v0:
```python
import jax
import jax.numpy as jnp
from jax import lax
from jax.sharding import PartitionSpec as P

eps = 1e-06


def padded_2(block, sides, width):
    for axis, dim in sides:
        count = lax.axis_size(axis)
        forward = [(i, i + 1) for i in range(count - 1)]
        backward = [(target, source) for source, target in forward]
        low = lax.ppermute(
            lax.slice_in_dim(block, block.shape[dim] - width, None, axis=dim), axis, forward
        )
        high = lax.ppermute(lax.slice_in_dim(block, 0, width, axis=dim), axis, backward)
        block = jnp.concatenate([low, block, high], axis=dim)
    return block


def depthwise(padded, weight, rows, cols):
    total = jnp.zeros((rows, cols, padded.shape[2]), jnp.float32)
    for tap_i in range(7):
        for tap_j in range(7):
            total = (
                total
                + padded[tap_i : tap_i + rows, tap_j : tap_j + cols] * weight[7 * tap_i + tap_j]
            )
    return total


def pointwise(conv, gain, w_up, w_down, grad_out, keep):
    mean = jnp.mean(conv, axis=-1, keepdims=True)
    centred = conv - mean
    inv = lax.rsqrt(jnp.mean(centred * centred, axis=-1, keepdims=True) + eps)
    normed = centred * inv
    scaled = (normed * gain).astype(jnp.bfloat16)
    hidden = jnp.dot(scaled, w_up, preferred_element_type=jnp.float32)
    act = (0.5 * hidden * (1.0 + lax.erf(hidden * 0.7071067811865476))).astype(jnp.bfloat16)
    grad_kept = grad_out * keep.astype(jnp.bfloat16)
    grad_down = lax.dot_general(
        act, grad_kept, (((0,), (0,)), ((), ())), preferred_element_type=jnp.float32
    )
    grad_act = lax.dot_general(
        grad_out, w_down, (((1,), (1,)), ((), ())), preferred_element_type=jnp.float32
    )
    slope = (
        0.5 * (1.0 + lax.erf(hidden * 0.7071067811865476))
        + hidden * jnp.exp(-0.5 * hidden * hidden) * 0.3989422804014327
    )
    grad_hidden = (grad_act * slope).astype(jnp.bfloat16)
    hidden_kept = grad_hidden * keep.astype(jnp.bfloat16)
    grad_up = lax.dot_general(
        scaled, hidden_kept, (((0,), (0,)), ((), ())), preferred_element_type=jnp.float32
    )
    grad_scaled = lax.dot_general(
        grad_hidden, w_up, (((1,), (1,)), ((), ())), preferred_element_type=jnp.float32
    )
    grad_gain = jnp.sum(grad_scaled * normed * keep, axis=0)
    g_norm = grad_scaled * gain
    grad_conv = inv * (
        g_norm
        - jnp.mean(g_norm, axis=-1, keepdims=True)
        - normed * jnp.mean(g_norm * normed, axis=-1, keepdims=True)
    )
    return (grad_conv.astype(jnp.bfloat16), grad_up, grad_down, grad_gain)


def on_device(features, dw_weight, norm_gain, w_up, w_down, cotangent):
    rows, cols, chans = features.shape
    padded = padded_2(features, (("rows", 0), ("cols", 1)), 3).astype(jnp.float32)
    conv = depthwise(padded, dw_weight, rows, cols)
    keep = jnp.ones((rows * cols, 1), jnp.float32)
    grad_flat, grad_up, grad_down, grad_gain = pointwise(
        conv.reshape(rows * cols, chans),
        norm_gain,
        w_up,
        w_down,
        cotangent.reshape(rows * cols, chans),
        keep,
    )
    grad_conv = grad_flat.reshape(rows, cols, chans)
    grad_wide = padded_2(grad_conv, (("rows", 0), ("cols", 1)), 3)
    grad_f = grad_conv.astype(jnp.float32)
    taps = []
    for tap_i in range(7):
        for tap_j in range(7):
            taps.append(
                jnp.sum(padded[tap_i : tap_i + rows, tap_j : tap_j + cols] * grad_f, axis=(0, 1))
            )
    grad_dw = jnp.stack(taps)
    grad_pad = grad_wide.astype(jnp.float32)
    total = cotangent.astype(jnp.float32)
    for tap_i in range(7):
        for tap_j in range(7):
            total = (
                total
                + grad_pad[6 - tap_i : 6 - tap_i + rows, 6 - tap_j : 6 - tap_j + cols]
                * dw_weight[7 * tap_i + tap_j]
            )
    grad_input = total.astype(jnp.bfloat16)
    grad_up, grad_down, grad_dw, grad_gain = lax.psum(
        (grad_up, grad_down, grad_dw, grad_gain), ("rows", "cols")
    )
    return (grad_input, grad_dw, grad_gain, grad_up, grad_down)


def solution(mesh):
    return jax.shard_map(
        on_device,
        mesh=mesh,
        in_specs=(P("rows", "cols", None), P(), P(), P(), P(), P("rows", "cols", None)),
        out_specs=(P("rows", "cols", None), P(), P(), P(), P()),
        check_vma=False,
    )
```

profile of v0, /device:TPU:0, one launch (start us, length us, event | category | flops | bytes accessed | tf_op | source)
XLA Modules:
  0.0 353.4 jit_solution(14381172907683778319)
XLA Ops:
  7.2 1.4 fusion.113
  8.6 4.9 %collective-permute-start = (bf16[3,128,512]{2,1,0:T(8,128)(2,1)S(1)}, bf16[3,128,512]{2,1,0:T(8,128)(2,1)S(1)}, u32[]{:S(2)}, u32[]{:S(2)}) collective-permute-start(bf16[3,128,512]{2,1,0:T(8,128)(2,1)S(1)} %get-tuple-element.70), channel_id=1, source_target_pairs={{0,4},{4,8},{8,12},{12,16},{16,20},{20,24},{24,28},{1,5},{5,9},{9,... | collective-permute-start | bytes 1179656 | tf_op jit(solution)/shard_map/ppermute | solution.py:14
  13.5 1.3 collective-permute-start.1
  16.1 1.2 fusion.115
  17.5 12.8 %collective-permute-done = bf16[3,128,512]{2,1,0:T(8,128)(2,1)S(1)} collective-permute-done((bf16[3,128,512]{2,1,0:T(8,128)(2,1)S(1)}, bf16[3,128,512]{2,1,0:T(8,128)(2,1)S(1)}, u32[]{:S(2)}, u32[]{:S(2)}) %collective-permute-start) | collective-permute-done | bytes 393248 | tf_op jit(solution)/shard_map/ppermute | solution.py:14
  30.5 1.3 collective-permute-start.3
  31.8 3.0 collective-permute-start.2
  34.9 1.6 fusion.116
  36.5 2.5 maximum_convert_fusion
  39.4 54.0 %fusion.110 = (f32[8,128]{1,0:T(8,128)S(1)}, f32[8,128,512]{2,1,0:T(8,128)}) fusion(f32[512]{0:T(512)} %bitcast.48, f32[14,134,512]{2,1,0:T(8,128)} %maximum_convert_fusion, f32[512]{0:T(512)} %bitcast.47, f32[512]{0:T(512)S(1)} %bitcast.183, f32[512]{0:T(512)S(1)} %bitcast.185, f32[512]{0:T(512)S(1)} %bitcast.187, f32[512]{0:T(512)S(1)} %bitcast.189, ...), kind=kLoop, calls=%fused_computation.231 | loop fusion | flops 51379200 | bytes 104962048 | tf_op jit(solution)/shard_map/reduce_sum | solution.py:34
  93.4 2.1 multiply_reduce_fusion.2
  96.0 2.3 fusion.117
  98.4 5.0 %fusion.5 = bf16[1024,2048]{1,0:T(8,128)(2,1)S(1)} fusion(f32[1024,2048]{1,0:T(8,128)S(1)} %fusion.117, bf16[1024,512]{1,0:T(8,128)(2,1)S(1)} %bitcast.179, bf16[2048,512]{1,0:T(8,128)(2,1)S(1)} %copy-done.48), kind=kOutput, calls=%fused_computation.55 | convolution fusion | flops 2168455168 | bytes 15728640 | tf_op jit(solution)/shard_map/dot_general | solution.py:45
  103.5 3.4 multiply_reduce_fusion
  107.1 6.6 %fusion.56 = (f32[512]{0:T(512)}, f32[512]{0:T(512)}, f32[512]{0:T(512)}, f32[512]{0:T(512)}, f32[512]{0:T(512)}, /*index=5*/f32[512]{0:T(512)}, f32[512]{0:T(51...) fusion(f32[14,134,512]{2,1,0:T(8,128)S(1)} %copy-done.1, ...), kind=kLoop, calls=%fused_computation.108 | loop fusion | flops 23583744 | bytes 43046912 | tf_op jit(solution)/shard_map/reduce_sum | solution.py:90
  114.7 4.0 %fusion.20 = (f32[512]{0:T(512)}, f32[512]{0:T(512)}, f32[512]{0:T(512)}, f32[512]{0:T(512)}, f32[512]{0:T(512)}, /*index=5*/f32[512]{0:T(512)}, f32[512]{0:T(51...) fusion(f32[14,134,512]{2,1,0:T(8,128)S(1)} %copy-done.1, ...), kind=kLoop, calls=%fused_computation.72 | loop fusion | flops 14149120 | bytes 28338176 | tf_op jit(solution)/shard_map/reduce_sum | solution.py:90
  118.7 5.3 %fusion.38 = (f32[512]{0:T(512)}, f32[512]{0:T(512)}, f32[512]{0:T(512)}, f32[512]{0:T(512)}, f32[512]{0:T(512)}, /*index=5*/f32[512]{0:T(512)}, f32[512]{0:T(51...) fusion(f32[14,134,512]{2,1,0:T(8,128)S(1)} %copy-done.1, ...), kind=kLoop, calls=%fused_computation.90 | loop fusion | flops 19389440 | bytes 38834176 | tf_op jit(solution)/shard_map/reduce_sum | solution.py:90
  124.0 6.1 %fusion.6 = f32[2048,512]{1,0:T(8,128)} fusion(bf16[1024,512]{1,0:T(8,128)(2,1)S(1)} %bitcast.180, f32[1024,2048]{1,0:T(8,128)} %copy-done.49), kind=kOutput, calls=%fused_computation.58 | convolution fusion | flops 2157969408 | bytes 13631488 | tf_op jit(solution)/shard_map/dot_general | solution.py:42
  130.1 1.3 collective-permute-start.5
  131.4 5.8 %collective-permute-start.4 = (bf16[3,128,512]{2,1,0:T(8,128)(2,1)}, bf16[3,128,512]{2,1,0:T(8,128)(2,1)}, u32[]{:S(2)}, u32[]{:S(2)}) collective-permute-start(bf16[3,128,512]{2,1,0:T(8,128)(2,1)} %bitcast.53), channel_id=1, source_target_pairs={{0,4},{4,8},{8,12},{12,16},{16,20},{20,24},{24,28},{1,5},{5,9},{9,... | collective-permute-start | bytes 1179656 | tf_op jit(solution)/shard_map/ppermute | solution.py:14
  137.2 9.4 %stack.199 = f32[49,512]{1,0:T(8,128)} concatenate(f32[1,512]{1,0:T(1,128)} %bitcast.315, f32[1,512]{1,0:T(1,128)} %bitcast.314, f32[1,512]{1,0:T(1,128)} %bitcast.313, f32[1,512]{1,0:T(1,128)} %bitcast.312, f32[1,512]{1,0:T(1,128)} %bitcast.311, f32[1,512]{1,0:T(1,128)} %bitcast.310, f32[1,512]{1,0:T(1,128)} %bitcast.309, f32[1,512]{1,0:T(1,128)} %bitcast.308, ...), dimensions={0} | concatenate | bytes 200704 | tf_op jit(solution)/shard_map/stack | solution.py:92
  146.5 6.9 %fusion.118 = f32[512,2048]{1,0:T(8,128)} fusion(bf16[1024,512]{1,0:T(8,128)(2,1)} %copy-done.4, bf16[1024,2048]{1,0:T(8,128)(2,1)} %copy-done.3), kind=kOutput, calls=%fused_computation.239 | convolution fusion | flops 2147483648 | bytes 9437184 | tf_op jit(solution)/shard_map/dot_general | solution.py:54
  153.6 1.4 pad_maximum_fusion.2
  155.1 1.3 collective-permute-start.7
  156.3 3.9 %collective-permute-start.6 = (bf16[14,3,512]{2,1,0:T(4,128)(2,1)}, bf16[14,3,512]{2,1,0:T(4,128)(2,1)}, u32[]{:S(2)}, u32[]{:S(2)}) collective-permute-start(bf16[14,3,512]{2,1,0:T(4,128)(2,1)} %get-tuple-element.63), channel_id=1, source_target_pairs={{0,1},{1,2},{2,3},{4,5},{5,6},{6,7},{8,9},{9,10},{10,11},{12,13},{... | collective-permute-start | bytes 129032 | tf_op jit(solution)/shard_map/ppermute | solution.py:14
  160.2 44.4 %psum.29 = f32[512]{0:T(512)} all-reduce(f32[512]{0:T(512)} %get-tuple-element.54), channel_id=1, replica_groups=mesh['rows'=8,'cols'=4] {'rows','cols'}, use_global_device_ids=true, to_apply=%region_55.0 | all-reduce | flops 512 | bytes 4096 | tf_op jit(solution)/shard_map/psum | solution.py:103
  204.6 3.6 %maximum_convert_fusion.1 = f32[14,134,512]{2,1,0:T(8,128)} fusion(bf16[14,3,512]{2,1,0:T(4,128)(2,1)} %collective-permute-done.7, bf16[3,128,512]{2,1,0:T(8,128)(2,1)S(1)} %collective-permute-done.5, bf16[8,128,512]{2,1,0:T(8,128)(2,1)S(1)} %bitcast.178, bf16[3,128,512]{2,1,0:T(8,128)(2,1)} %collective-permute-done.4, ...), kind=kLoop, calls=%fused_computation.217 | loop fusion | flops 9605120 | bytes 5763072 | tf_op jit(solution)/shard_map/convert_element_type | solution.py:93
  208.1 52.3 %fusion.58 = bf16[8,128,512]{2,1,0:T(8,128)(2,1)} fusion(f32[14,134,512]{2,1,0:T(8,128)} %maximum_convert_fusion.1, bf16[8,128,512]{2,1,0:T(8,128)(2,1)} %param.11, f32[512]{0:T(512)} %bitcast.48, f32[512]{0:T(512)} %bitcast.47, f32[512]{0:T(512)S(1)} %bitcast.184, f32[512]{0:T(512)S(1)} %bitcast.186, f32[512]{0:T(512)S(1)} %bitcast.188, f32[512]{0:T(512)} %bitcast.190, ...), kind=kLoop, calls=%fused_computation.111 | loop fusion | flops 52428800 | bytes 104957952 | tf_op jit(solution)/shard_map/convert_element_type | solution.py:102
  260.4 77.8 %all-reduce.3.cloned.1.call-done = (f32[49,512]{1,0:T(8,128)}, f32[512,2048]{1,0:T(8,128)}, f32[2048,512]{1,0:T(8,128)}) async-done(((f32[49,512]{1,0:T(8,128)}, f32[512,2048]{1,0:T(8,128)}, f32[2048,512]{1,0:T(8,128)}), (f32[49,512]{1,0:T(8,128)}, f32[512,2048]{1,0:T(8,128)}, f32[2048,512]{1,0:T(8,128)})) %all-reduce.3.cloned.1.call-update) | async-done | bytes 8488976 | tf_op jit(solution)/shard_map/psum | solution.py:103
  338.2 1.6 copy.16
  339.7 4.8 %copy.17 = f32[512,2048]{1,0:T(8,128)} copy(f32[512,2048]{1,0:T(8,128)} %get-tuple-element.128) | data formatting | bytes 8388608
  344.6 2.0 copy.18
  (119 shorter events, 3.4 us)
Async XLA Ops:
  7.2 88.8 %copy-start = (bf16[512,2048]{1,0:T(8,128)(2,1)S(1)}, bf16[512,2048]{1,0:T(8,128)(2,1)}, u32[]{:S(2)}) copy-start(bf16[512,2048]{1,0:T(8,128)(2,1)} %param.9) | copy-start | bytes 6291460
  7.2 23.1 %copy-start.6 = (bf16[8,128,512]{2,1,0:T(8,128)(2,1)S(1)}, bf16[8,128,512]{2,1,0:T(8,128)(2,1)}, u32[]{:S(2)}) copy-start(bf16[8,128,512]{2,1,0:T(8,128)(2,1)} %param.6) | copy-start | bytes 3145732
  7.2 331.0 %all-reduce.3.cloned.1.call-start = ((), (), s32[]{:S(2)}) async-start(), calls=%async_computation | async-start | bytes 17006592 | tf_op jit(solution)/shard_map/psum | solution.py:103
  8.6 21.7 %collective-permute-start = (bf16[3,128,512]{2,1,0:T(8,128)(2,1)S(1)}, bf16[3,128,512]{2,1,0:T(8,128)(2,1)S(1)}, u32[]{:S(2)}, u32[]{:S(2)}) collective-permute-start(bf16[3,128,512]{2,1,0:T(8,128)(2,1)S(1)} %get-tuple-element.70), channel_id=1, source_target_pairs={{0,4},{4,8},{8,12},{12,16},{16,20},{20,24},{24,28},{1,5},{5,9},{9,... | collective-permute-start | bytes 1179656 | tf_op jit(solution)/shard_map/ppermute | solution.py:14
  13.5 16.9 %collective-permute-start.1 = (bf16[3,128,512]{2,1,0:T(8,128)(2,1)S(1)}, bf16[3,128,512]{2,1,0:T(8,128)(2,1)S(1)}, u32[]{:S(2)}, u32[]{:S(2)}) collective-permute-start(bf16[3,128,512]{2,1,0:T(8,128)(2,1)S(1)} %get-tuple-element.69), channel_id=1, source_target_pairs={{4,0},{8,4},{12,8},{16,12},{20,16},{24,20},{28,24},{5,1},{9,5},{13... | collective-permute-start | bytes 1179656 | tf_op jit(solution)/shard_map/ppermute | solution.py:17
  16.0 23.1 %copy-start.8 = (f32[1,512]{1,0:T(1,128)}, f32[1,512]{1,0:T(1,128)S(1)}, u32[]{:S(2)}) copy-start(f32[1,512]{1,0:T(1,128)S(1)} %get-tuple-element.75) | copy-start | bytes 6148
  16.0 23.1 %copy-start.9 = (f32[1,512]{1,0:T(1,128)}, f32[1,512]{1,0:T(1,128)S(1)}, u32[]{:S(2)}) copy-start(f32[1,512]{1,0:T(1,128)S(1)} %get-tuple-element.76) | copy-start | bytes 6148
  16.0 23.1 %copy-start.10 = (f32[1,512]{1,0:T(1,128)}, f32[1,512]{1,0:T(1,128)S(1)}, u32[]{:S(2)}) copy-start(f32[1,512]{1,0:T(1,128)S(1)} %get-tuple-element.77) | copy-start | bytes 6148
  16.0 23.1 %copy-start.11 = (f32[1,512]{1,0:T(1,128)}, f32[1,512]{1,0:T(1,128)S(1)}, u32[]{:S(2)}) copy-start(f32[1,512]{1,0:T(1,128)S(1)} %get-tuple-element.78) | copy-start | bytes 6148
  16.0 23.1 %copy-start.12 = (f32[1,512]{1,0:T(1,128)}, f32[1,512]{1,0:T(1,128)S(1)}, u32[]{:S(2)}) copy-start(f32[1,512]{1,0:T(1,128)S(1)} %get-tuple-element.79) | copy-start | bytes 6148
  16.0 23.1 %copy-start.13 = (f32[1,512]{1,0:T(1,128)}, f32[1,512]{1,0:T(1,128)S(1)}, u32[]{:S(2)}) copy-start(f32[1,512]{1,0:T(1,128)S(1)} %get-tuple-element.80) | copy-start | bytes 6148
  16.0 23.1 %copy-start.14 = (f32[1,512]{1,0:T(1,128)}, f32[1,512]{1,0:T(1,128)S(1)}, u32[]{:S(2)}) copy-start(f32[1,512]{1,0:T(1,128)S(1)} %get-tuple-element.81) | copy-start | bytes 6148
  16.0 23.1 %copy-start.15 = (f32[1,512]{1,0:T(1,128)}, f32[1,512]{1,0:T(1,128)S(1)}, u32[]{:S(2)}) copy-start(f32[1,512]{1,0:T(1,128)S(1)} %get-tuple-element.82) | copy-start | bytes 6148
  16.0 23.1 %copy-start.16 = (f32[1,512]{1,0:T(1,128)}, f32[1,512]{1,0:T(1,128)S(1)}, u32[]{:S(2)}) copy-start(f32[1,512]{1,0:T(1,128)S(1)} %get-tuple-element.83) | copy-start | bytes 6148
  16.0 23.1 %copy-start.17 = (f32[1,512]{1,0:T(1,128)}, f32[1,512]{1,0:T(1,128)S(1)}, u32[]{:S(2)}) copy-start(f32[1,512]{1,0:T(1,128)S(1)} %get-tuple-element.84) | copy-start | bytes 6148
  16.1 23.1 %copy-start.18 = (f32[1,512]{1,0:T(1,128)}, f32[1,512]{1,0:T(1,128)S(1)}, u32[]{:S(2)}) copy-start(f32[1,512]{1,0:T(1,128)S(1)} %get-tuple-element.85) | copy-start | bytes 6148
  16.1 23.1 %copy-start.19 = (f32[1,512]{1,0:T(1,128)}, f32[1,512]{1,0:T(1,128)S(1)}, u32[]{:S(2)}) copy-start(f32[1,512]{1,0:T(1,128)S(1)} %get-tuple-element.86) | copy-start | bytes 6148
  16.1 23.1 %copy-start.20 = (f32[1,512]{1,0:T(1,128)}, f32[1,512]{1,0:T(1,128)S(1)}, u32[]{:S(2)}) copy-start(f32[1,512]{1,0:T(1,128)S(1)} %get-tuple-element.87) | copy-start | bytes 6148
  16.1 23.1 %copy-start.21 = (f32[1,512]{1,0:T(1,128)}, f32[1,512]{1,0:T(1,128)S(1)}, u32[]{:S(2)}) copy-start(f32[1,512]{1,0:T(1,128)S(1)} %get-tuple-element.88) | copy-start | bytes 6148
  16.1 23.1 %copy-start.22 = (f32[1,512]{1,0:T(1,128)}, f32[1,512]{1,0:T(1,128)S(1)}, u32[]{:S(2)}) copy-start(f32[1,512]{1,0:T(1,128)S(1)} %get-tuple-element.89) | copy-start | bytes 6148
  17.3 21.9 %copy-start.23 = (f32[1,512]{1,0:T(1,128)}, f32[1,512]{1,0:T(1,128)S(1)}, u32[]{:S(2)}) copy-start(f32[1,512]{1,0:T(1,128)S(1)} %get-tuple-element.90) | copy-start | bytes 6148
  17.3 21.9 %copy-start.24 = (f32[1,512]{1,0:T(1,128)}, f32[1,512]{1,0:T(1,128)S(1)}, u32[]{:S(2)}) copy-start(f32[1,512]{1,0:T(1,128)S(1)} %get-tuple-element.91) | copy-start | bytes 6148
  17.3 21.9 %copy-start.25 = (f32[1,512]{1,0:T(1,128)}, f32[1,512]{1,0:T(1,128)S(1)}, u32[]{:S(2)}) copy-start(f32[1,512]{1,0:T(1,128)S(1)} %get-tuple-element.92) | copy-start | bytes 6148
  17.3 21.9 %copy-start.26 = (f32[1,512]{1,0:T(1,128)}, f32[1,512]{1,0:T(1,128)S(1)}, u32[]{:S(2)}) copy-start(f32[1,512]{1,0:T(1,128)S(1)} %get-tuple-element.93) | copy-start | bytes 6148
  17.3 21.9 %copy-start.27 = (f32[1,512]{1,0:T(1,128)}, f32[1,512]{1,0:T(1,128)S(1)}, u32[]{:S(2)}) copy-start(f32[1,512]{1,0:T(1,128)S(1)} %get-tuple-element.94) | copy-start | bytes 6148
  17.3 21.9 %copy-start.28 = (f32[1,512]{1,0:T(1,128)}, f32[1,512]{1,0:T(1,128)S(1)}, u32[]{:S(2)}) copy-start(f32[1,512]{1,0:T(1,128)S(1)} %get-tuple-element.95) | copy-start | bytes 6148
  30.5 6.0 %collective-permute-start.3 = (bf16[14,3,512]{2,1,0:T(4,128)(2,1)S(1)}, bf16[14,3,512]{2,1,0:T(4,128)(2,1)S(1)}, u32[]{:S(2)}, u32[]{:S(2)}) collective-permute-start(bf16[14,3,512]{2,1,0:T(4,128)(2,1)S(1)} %get-tuple-element.66), channel_id=1, source_target_pairs={{1,0},{2,1},{3,2},{5,4},{6,5},{7,6},{9,8},{10,9},{11,10},{13,12},{... | collective-permute-start | bytes 129032 | tf_op jit(solution)/shard_map/ppermute | solution.py:17
  31.8 4.7 %collective-permute-start.2 = (bf16[14,3,512]{2,1,0:T(4,128)(2,1)S(1)}, bf16[14,3,512]{2,1,0:T(4,128)(2,1)S(1)}, u32[]{:S(2)}, u32[]{:S(2)}) collective-permute-start(bf16[14,3,512]{2,1,0:T(4,128)(2,1)S(1)} %get-tuple-element.65), channel_id=1, source_target_pairs={{0,1},{1,2},{2,3},{4,5},{5,6},{6,7},{8,9},{9,10},{10,11},{12,13},{... | collective-permute-start | bytes 129032 | tf_op jit(solution)/shard_map/ppermute | solution.py:14
  130.1 23.3 %collective-permute-start.5 = (bf16[3,128,512]{2,1,0:T(8,128)(2,1)}, bf16[3,128,512]{2,1,0:T(8,128)(2,1)S(1)}, u32[]{:S(2)}, u32[]{:S(2)}) collective-permute-start(bf16[3,128,512]{2,1,0:T(8,128)(2,1)} %bitcast.55), channel_id=1, source_target_pairs={{4,0},{8,4},{12,8},{16,12},{20,16},{24,20},{28,24},{5,1},{9,5},{13... | collective-permute-start | bytes 1179656 | tf_op jit(solution)/shard_map/ppermute | solution.py:17
  131.4 22.2 %collective-permute-start.4 = (bf16[3,128,512]{2,1,0:T(8,128)(2,1)}, bf16[3,128,512]{2,1,0:T(8,128)(2,1)}, u32[]{:S(2)}, u32[]{:S(2)}) collective-permute-start(bf16[3,128,512]{2,1,0:T(8,128)(2,1)} %bitcast.53), channel_id=1, source_target_pairs={{0,4},{4,8},{8,12},{12,16},{16,20},{20,24},{24,28},{1,5},{5,9},{9,... | collective-permute-start | bytes 1179656 | tf_op jit(solution)/shard_map/ppermute | solution.py:14
  155.1 49.5 %collective-permute-start.7 = (bf16[14,3,512]{2,1,0:T(4,128)(2,1)}, bf16[14,3,512]{2,1,0:T(4,128)(2,1)}, u32[]{:S(2)}, u32[]{:S(2)}) collective-permute-start(bf16[14,3,512]{2,1,0:T(4,128)(2,1)} %get-tuple-element.64), channel_id=1, source_target_pairs={{1,0},{2,1},{3,2},{5,4},{6,5},{7,6},{9,8},{10,9},{11,10},{13,12},{... | collective-permute-start | bytes 129032 | tf_op jit(solution)/shard_map/ppermute | solution.py:17
  156.3 48.2 %collective-permute-start.6 = (bf16[14,3,512]{2,1,0:T(4,128)(2,1)}, bf16[14,3,512]{2,1,0:T(4,128)(2,1)}, u32[]{:S(2)}, u32[]{:S(2)}) collective-permute-start(bf16[14,3,512]{2,1,0:T(4,128)(2,1)} %get-tuple-element.63), channel_id=1, source_target_pairs={{0,1},{1,2},{2,3},{4,5},{5,6},{6,7},{8,9},{9,10},{10,11},{12,13},{... | collective-permute-start | bytes 129032 | tf_op jit(solution)/shard_map/ppermute | solution.py:14
  (27 other events, 327.8 us)
Sparse Core Ops, SparseCore 0:
  153.6 184.5 all-reduce.2
where the time goes:
time: 354 us; the launch traced here: 353 us
  other arithmetic  132 us (37%)
  waiting for transfers between devices  90.8 us (26%)
  blocking collectives  44.4 us (13%)
  local copies, waits for them, and re-layouts  24.7 us (7%)
  matrix products  23.8 us (7%)
  starting transfers between devices  22.8 us (6%)
  between operations  14.9 us (4%)
    psum x1, waiting for transfers between devices, on_device(): lax.psum((grad_up, grad_down, grad_dw, grad_gain), ('rows', 'cols'))  77.8 us
    reduce_sum x1, other arithmetic, pointwise(): mean = jnp.mean(conv, axis=-1, keepdims=True)  54 us
    convert_element_type x1, other arithmetic, on_device(): grad_input = total.astype(jnp.bfloat16)  52.3 us
    psum x1, blocking collectives, on_device(): lax.psum((grad_up, grad_down, grad_dw, grad_gain), ('rows', 'cols'))  44.4 us
    ppermute x4, starting transfers between devices, padded_2(): lax.ppermute(lax.slice_in_dim(block, block.shape[dim] - width, None, axis...  17.6 us
    reduce_sum x3, other arithmetic, on_device(): jnp.sum(padded[tap_i:tap_i + rows, tap_j:tap_j + cols] * grad_f, axis=(0,...  15.9 us
    ppermute x4, waiting for transfers between devices, padded_2(): lax.ppermute(lax.slice_in_dim(block, block.shape[dim] - width, None, axis...  13 us
    another operation x1, local copies, waits for them, and re-layouts, on_device(): grad_dw = jnp.stack(taps)  9.36 us
  transfers between devices with their start and end apart: 9, of which 3 were waited for; matrix products, arithmetic and copies ran while one was open for 22% of the time, Pallas kernels for 0%

commit v1 on v0

v1 whole, which is shorter than its diff:
```python
import jax
import jax.numpy as jnp
from jax import lax
from jax.experimental import pallas as pl
from jax.experimental.pallas import tpu as pltpu
from jax.sharding import PartitionSpec as P

eps = 1e-06

LANES = 128
STEP = 16


def conv_kernel(has_base, *refs):
    if has_base:
        x_ref, w_ref, base_ref, out_ref, wide, taps = refs
    else:
        x_ref, w_ref, out_ref, wide, taps = refs
    rows, cols, _ = out_ref.shape
    wide[...] = x_ref[...].astype(jnp.float32)
    for k in range(49):
        taps[k] = jnp.broadcast_to(w_ref[k : k + 1, :], (8, LANES))

    def step(c, carry):
        at = pl.multiple_of(c * STEP, STEP)
        if has_base:
            acc = [base_ref[r, pl.ds(at, STEP), :].astype(jnp.float32) for r in range(rows)]
        else:
            acc = [None] * rows
        for j in range(7):
            weights = [jnp.concatenate([taps[7 * i + j]] * 2, axis=0) for i in range(7)]
            for r in range(rows + 6):
                x = wide[r, pl.ds(at + j, STEP), :]
                for i in range(7):
                    if 0 <= r - i < rows:
                        term = x * weights[i]
                        acc[r - i] = term if acc[r - i] is None else acc[r - i] + term
        for r in range(rows):
            out_ref[r, pl.ds(at, STEP), :] = acc[r].astype(out_ref.dtype)
        return carry

    lax.fori_loop(0, cols // STEP, step, 0)


def dw_kernel(x_ref, g_ref, out_ref, wide, sums):
    rows, cols, _ = g_ref.shape
    wide[...] = x_ref[...].astype(jnp.float32)
    sums[...] = jnp.zeros_like(sums)

    def step(c, carry):
        at = pl.multiple_of(c * STEP, STEP)
        grad = [g_ref[r, pl.ds(at, STEP), :].astype(jnp.float32) for r in range(rows)]
        for j in range(7):
            acc = [sums[7 * i + j] for i in range(7)]
            for r in range(rows + 6):
                x = wide[r, pl.ds(at + j, STEP), :]
                for i in range(7):
                    if 0 <= r - i < rows:
                        term = x * grad[r - i]
                        acc[i] = acc[i] + (term[:8] + term[8:])
            for i in range(7):
                sums[7 * i + j] = acc[i]
        return carry

    lax.fori_loop(0, cols // STEP, step, 0)
    for k in range(49):
        out_ref[k : k + 1, :] = jnp.sum(sums[k], axis=0, keepdims=True)


def block3(shape):
    return pl.BlockSpec((shape[0], shape[1], LANES), lambda c: (0, 0, c))


def depthwise(wide, weight, rows, cols, base=None):
    chans = wide.shape[2]
    args = [wide, weight] + ([] if base is None else [base])
    specs = [block3(wide.shape), pl.BlockSpec((49, LANES), lambda c: (0, c))]
    if base is not None:
        specs.append(block3(base.shape))
    kind = jnp.float32 if base is None else jnp.bfloat16
    return pl.pallas_call(
        lambda *refs: conv_kernel(base is not None, *refs),
        grid=(chans // LANES,),
        in_specs=specs,
        out_specs=block3((rows, cols)),
        out_shape=jax.ShapeDtypeStruct((rows, cols, chans), kind),
        scratch_shapes=[
            pltpu.VMEM((wide.shape[0], wide.shape[1], LANES), jnp.float32),
            pltpu.VMEM((49, 8, LANES), jnp.float32),
        ],
        cost_estimate=pl.CostEstimate(
            flops=100 * rows * cols * chans, bytes_accessed=4 * rows * cols * chans, transcendentals=0
        ),
        name="conv",
    )(*args)


def depthwise_grad(wide, grad):
    rows, cols, chans = grad.shape
    return pl.pallas_call(
        dw_kernel,
        grid=(chans // LANES,),
        in_specs=[block3(wide.shape), block3(grad.shape)],
        out_specs=pl.BlockSpec((49, LANES), lambda c: (0, c)),
        out_shape=jax.ShapeDtypeStruct((49, chans), jnp.float32),
        scratch_shapes=[
            pltpu.VMEM((wide.shape[0], wide.shape[1], LANES), jnp.float32),
            pltpu.VMEM((49, 8, LANES), jnp.float32),
        ],
        cost_estimate=pl.CostEstimate(
            flops=100 * rows * cols * chans, bytes_accessed=4 * rows * cols * chans, transcendentals=0
        ),
        name="dw",
    )(wide, grad)


def padded_2(block, sides, width):
    for axis, dim in sides:
        count = lax.axis_size(axis)
        forward = [(i, i + 1) for i in range(count - 1)]
        backward = [(target, source) for source, target in forward]
        low = lax.ppermute(
            lax.slice_in_dim(block, block.shape[dim] - width, None, axis=dim), axis, forward
        )
        high = lax.ppermute(lax.slice_in_dim(block, 0, width, axis=dim), axis, backward)
        block = jnp.concatenate([low, block, high], axis=dim)
    return block


def pointwise(conv, gain, w_up, w_down, grad_out):
    mean = jnp.mean(conv, axis=-1, keepdims=True)
    centred = conv - mean
    inv = lax.rsqrt(jnp.mean(centred * centred, axis=-1, keepdims=True) + eps)
    normed = centred * inv
    scaled = (normed * gain).astype(jnp.bfloat16)
    hidden = jnp.dot(scaled, w_up, preferred_element_type=jnp.float32)
    act = (0.5 * hidden * (1.0 + lax.erf(hidden * 0.7071067811865476))).astype(jnp.bfloat16)
    grad_down = lax.dot_general(
        act, grad_out, (((0,), (0,)), ((), ())), preferred_element_type=jnp.float32
    )
    grad_act = lax.dot_general(
        grad_out, w_down, (((1,), (1,)), ((), ())), preferred_element_type=jnp.float32
    )
    slope = (
        0.5 * (1.0 + lax.erf(hidden * 0.7071067811865476))
        + hidden * jnp.exp(-0.5 * hidden * hidden) * 0.3989422804014327
    )
    grad_hidden = (grad_act * slope).astype(jnp.bfloat16)
    grad_up = lax.dot_general(
        scaled, grad_hidden, (((0,), (0,)), ((), ())), preferred_element_type=jnp.float32
    )
    grad_scaled = lax.dot_general(
        grad_hidden, w_up, (((1,), (1,)), ((), ())), preferred_element_type=jnp.float32
    )
    grad_gain = jnp.sum(grad_scaled * normed, axis=0)
    g_norm = grad_scaled * gain
    grad_conv = inv * (
        g_norm
        - jnp.mean(g_norm, axis=-1, keepdims=True)
        - normed * jnp.mean(g_norm * normed, axis=-1, keepdims=True)
    )
    return (grad_conv.astype(jnp.bfloat16), grad_up, grad_down, grad_gain)


def on_device(features, dw_weight, norm_gain, w_up, w_down, cotangent):
    rows, cols, chans = features.shape
    extra = -(cols + 6) % STEP

    def widened(block):
        return jnp.pad(
            padded_2(block, (("rows", 0), ("cols", 1)), 3), ((0, 0), (0, extra), (0, 0))
        )

    padded = widened(features)
    conv = depthwise(padded, dw_weight, rows, cols)
    grad_flat, grad_up, grad_down, grad_gain = pointwise(
        conv.reshape(rows * cols, chans),
        norm_gain,
        w_up,
        w_down,
        cotangent.reshape(rows * cols, chans),
    )
    grad_down = lax.psum(grad_down.astype(jnp.bfloat16), ("rows", "cols"))
    grad_conv = grad_flat.reshape(rows, cols, chans)
    grad_dw = depthwise_grad(padded, grad_conv)
    small = jnp.concatenate([grad_dw, grad_gain[None]], axis=0)
    grad_up, small = lax.psum(
        (grad_up.astype(jnp.bfloat16), small.astype(jnp.bfloat16)), ("rows", "cols")
    )
    grad_input = depthwise(widened(grad_conv), dw_weight[::-1], rows, cols, cotangent)
    small = small.astype(jnp.float32)
    return (
        grad_input,
        small[:49],
        small[49],
        grad_up.astype(jnp.float32),
        grad_down.astype(jnp.float32),
    )


def solution(mesh):
    return jax.shard_map(
        on_device,
        mesh=mesh,
        in_specs=(P("rows", "cols", None), P(), P(), P(), P(), P("rows", "cols", None)),
        out_specs=(P("rows", "cols", None), P(), P(), P(), P()),
        check_vma=False,
    )
```

time: 354 us -> 240 us (0.68)
  other arithmetic: 132 us -> 20.8 us
  Pallas kernels: 0 us -> 32.8 us
  waiting for transfers between devices: 90.8 us -> 76.2 us
  local copies, waits for them, and re-layouts: 24.7 us -> 10.2 us
    reduce_sum x1, other arithmetic: 54 us -> 1.81 us  [pointwise(): mean = jnp.mean(conv, axis=-1, keepdims=True)]
    convert_element_type x3, other arithmetic: 58.4 us -> 7.95 us  [the longest x1 4.28 us: on_device(): grad_up.astype(jnp.float32)]
    pallas_call x0 -> x3, Pallas kernels: none -> 32.8 us  [the longest x2 23.5 us: depthwise(): pl.pallas_call(lambda *refs: conv_kernel(base is not None, *refs), grid=(...]
    psum x1, waiting for transfers between devices: 77.8 us -> 50.2 us  [on_device(): lax.psum((grad_up.astype(jnp.bfloat16), small.astype(jnp.bfloat16)), ('ro...]
    reduce_sum x3 -> x0, other arithmetic: 15.9 us -> none  [on_device(): jnp.sum(padded[tap_i:tap_i + rows, tap_j:tap_j + cols] * grad_f, axis=(0,...]
    ppermute x4, waiting for transfers between devices: 13 us -> 22.5 us  [padded_2(): lax.ppermute(lax.slice_in_dim(block, block.shape[dim] - width, None, axis...]
    another operation x1 -> x0, local copies, waits for them, and re-layouts: 9.36 us -> none  [on_device(): grad_dw = jnp.stack(taps)]
    unnamed x105 -> x24, local copies, waits for them, and re-layouts: 9.05 us -> 2.24 us
  transfers between devices with their start and end apart: 9 -> 9, of which waited for: 3 -> 4; matrix products, arithmetic and copies ran while one was open for 22% -> 8% of each run, Pallas kernels for 0% -> 8%
where the time goes in v1:
time: 240 us; the launch traced here: 239 us
  waiting for transfers between devices  76.2 us (32%)
  blocking collectives  43.4 us (18%)
  Pallas kernels  32.8 us (14%)
  matrix products  20.9 us (9%)
  other arithmetic  20.8 us (9%)
  starting transfers between devices  20.5 us (9%)
  between operations  14.3 us (6%)
  local copies, waits for them, and re-layouts  10.2 us (4%)
    psum x1, waiting for transfers between devices, on_device(): lax.psum((grad_up.astype(jnp.bfloat16), small.astype(jnp.bfloat16)), ('ro...  50.2 us
    psum x1, blocking collectives, on_device(): lax.psum((grad_up.astype(jnp.bfloat16), small.astype(jnp.bfloat16)), ('ro...  43.4 us
    pallas_call x2, Pallas kernels, depthwise(): pl.pallas_call(lambda *refs: conv_kernel(base is not None, *refs), grid=(...  23.5 us
    ppermute x4, waiting for transfers between devices, padded_2(): lax.ppermute(lax.slice_in_dim(block, block.shape[dim] - width, None, axis...  22.5 us
    ppermute x4, starting transfers between devices, padded_2(): lax.ppermute(lax.slice_in_dim(block, block.shape[dim] - width, None, axis...  15.4 us
    pallas_call x1, Pallas kernels, depthwise_grad(): pl.pallas_call(dw_kernel, grid=(chans // LANES,), in_specs=[block3(wide.s...  9.29 us
    dot_general x1, matrix products, pointwise(): lax.dot_general(grad_hidden, w_up, (((1,), (1,)), ((), ())), preferred_el...  5.78 us
    concatenate x2, other arithmetic, padded_2(): block = jnp.concatenate([low, block, high], axis=dim)  5.34 us
  transfers between devices with their start and end apart: 9, of which 4 were waited for; matrix products, arithmetic and copies ran while one was open for 8% of the time, Pallas kernels for 8%

profile of v1, /device:TPU:0, one launch (start us, length us, event | category | flops | bytes accessed | tf_op | source)
XLA Modules:
  0.0 239.2 jit_solution(10729970542167353772)
XLA Ops:
  7.2 1.4 fusion.28
  8.6 4.9 %collective-permute-start = (bf16[3,128,512]{2,1,0:T(8,128)(2,1)S(1)}, bf16[3,128,512]{2,1,0:T(8,128)(2,1)S(1)}, u32[]{:S(2)}, u32[]{:S(2)}) collective-permute-start(bf16[3,128,512]{2,1,0:T(8,128)(2,1)S(1)} %get-tuple-element.17), channel_id=1, source_target_pairs={{0,4},{4,8},{8,12},{12,16},{16,20},{20,24},{24,28},{1,5},{5,9},{9,... | collective-permute-start | bytes 1179656 | tf_op jit(solution)/shard_map/ppermute | solution.py:122
  13.5 1.3 collective-permute-start.1
  14.8 15.5 %collective-permute-done = bf16[3,128,512]{2,1,0:T(8,128)(2,1)S(1)} collective-permute-done((bf16[3,128,512]{2,1,0:T(8,128)(2,1)S(1)}, bf16[3,128,512]{2,1,0:T(8,128)(2,1)S(1)}, u32[]{:S(2)}, u32[]{:S(2)}) %collective-permute-start) | collective-permute-done | bytes 393248 | tf_op jit(solution)/shard_map/ppermute | solution.py:122
  30.5 1.3 collective-permute-start.2
  31.9 1.3 collective-permute-start.3
  33.2 3.5 %collective-permute-done.3 = bf16[14,3,512]{2,1,0:T(4,128)(2,1)S(1)} collective-permute-done((bf16[14,3,512]{2,1,0:T(4,128)(2,1)S(1)}, bf16[14,3,512]{2,1,0:T(4,128)(2,1)S(1)}, u32[]{:S(2)}, u32[]{:S(2)}) %collective-permute-start.3) | collective-permute-done | bytes 43040 | tf_op jit(solution)/shard_map/ppermute | solution.py:125
  36.7 2.3 fusion.21.refs_0_.x_ref
  39.0 12.7 %conv.2 = f32[8,128,512]{2,1,0:T(8,128)} custom-call(bf16[14,144,512]{2,1,0:T(8,128)(2,1)} %fusion.21.refs_0_.x_ref, f32[49,512]{1,0:T(8,128)} %refs_1_.1), custom_call_target="tpu_custom_call" | custom-call | flops 52428800 | bytes 2097152 | tf_op jit(solution)/shard_map/conv/pallas_call | solution.py:81
  51.7 1.8 reduce_sum.45
  53.6 2.1 multiply_reduce_fusion.2
  56.2 2.3 fusion.29
  58.5 4.0 %fusion.16 = bf16[2048,512]{1,0:T(8,128)(2,1)} fusion(bf16[1024,512]{1,0:T(8,128)(2,1)S(1)} %bitcast.33, f32[1024,2048]{1,0:T(8,128)S(1)} %fusion.29), kind=kOutput, calls=%fused_computation.21 | convolution fusion | flops 2159017984 | bytes 11534336 | tf_op jit(solution)/shard_map/dot_general | solution.py:138
  62.5 5.0 %fusion.5 = bf16[1024,2048]{1,0:T(8,128)(2,1)S(1)} fusion(f32[1024,2048]{1,0:T(8,128)S(1)} %fusion.29, bf16[1024,512]{1,0:T(8,128)(2,1)S(1)} %bitcast.34, bf16[2048,512]{1,0:T(8,128)(2,1)S(1)} %copy-done.9), kind=kOutput, calls=%fused_computation.6 | convolution fusion | flops 2168455168 | bytes 15728640 | tf_op jit(solution)/shard_map/dot_general | solution.py:141
  67.6 2.0 copy-done.10
  69.6 3.8 %convolution_convert_fusion = bf16[512,2048]{1,0:T(8,128)(2,1)} fusion(bf16[1024,512]{1,0:T(8,128)(2,1)S(1)} %multiply_convert_fusion.5, bf16[1024,2048]{1,0:T(8,128)(2,1)S(1)} %fusion.5), kind=kOutput, calls=%fused_computation.20 | convolution fusion | flops 2148532224 | bytes 7340032 | tf_op jit(solution)/shard_map/dot_general | solution.py:149
  73.4 5.8 %multiply_reduce_fusion = (bf16[512]{0:T(512)(128)(2,1)S(1)}, f32[1024]{0:T(1024)S(1)}, f32[1024]{0:T(1024)S(1)}, f32[1024,512]{1,0:T(8,128)S(1)}) fusion(f32[8,128,512]{2,1,0:T(8,128)} %conv.2, f32[1024]{0:T(1024)S(1)} %get-tuple-element.19, f32[1024]{0:T(1024)S(1)} %rsqrt_bitcast_fusion, f32[512]{0:T(512)S(1)} %copy-done.8, ...), kind=kOutput, calls=%fused_computation.24 | convolution fusion | flops 2151675392 | bytes 10505216 | tf_op jit(solution)/shard_map/dot_general | solution.py:152
  81.3 1.3 collective-permute-start.5
  82.6 6.0 %collective-permute-start.4 = (bf16[3,128,512]{2,1,0:T(8,128)(2,1)}, bf16[3,128,512]{2,1,0:T(8,128)(2,1)}, u32[]{:S(2)}, u32[]{:S(2)}) collective-permute-start(bf16[3,128,512]{2,1,0:T(8,128)(2,1)} %bitcast.4), channel_id=1, source_target_pairs={{0,4},{4,8},{8,12},{12,16},{16,20},{20,24},{24,28},{1,5},{5,9},{9,... | collective-permute-start | bytes 1179656 | tf_op jit(solution)/shard_map/ppermute | solution.py:122
  88.6 2.7 %rev.3.refs_1_ = f32[49,512]{1,0:T(8,128)} reverse(f32[49,512]{1,0:T(8,128)} %refs_1_.1), dimensions={0} | reverse | bytes 200704 | tf_op jit(solution)/shard_map/rev | solution.py:190
  91.3 9.3 %dw.1 = f32[49,512]{1,0:T(8,128)} custom-call(bf16[14,144,512]{2,1,0:T(8,128)(2,1)} %fusion.21.refs_0_.x_ref, bf16[8,128,512]{2,1,0:T(8,128)(2,1)} %bitcast.30), custom_call_target="tpu_custom_call" | custom-call | flops 52428800 | bytes 2097152 | tf_op jit(solution)/shard_map/dw/pallas_call | solution.py:100
  101.7 7.0 %collective-permute-done.4 = bf16[3,128,512]{2,1,0:T(8,128)(2,1)} collective-permute-done((bf16[3,128,512]{2,1,0:T(8,128)(2,1)}, bf16[3,128,512]{2,1,0:T(8,128)(2,1)}, u32[]{:S(2)}, u32[]{:S(2)}) %collective-permute-start.4) | collective-permute-done | bytes 393248 | tf_op jit(solution)/shard_map/ppermute | solution.py:122
  108.7 1.6 pad_maximum_fusion.2
  110.3 3.1 %collective-permute-start.6 = (bf16[14,3,512]{2,1,0:T(4,128)(2,1)}, bf16[14,3,512]{2,1,0:T(4,128)(2,1)}, u32[]{:S(2)}, u32[]{:S(2)}) collective-permute-start(bf16[14,3,512]{2,1,0:T(4,128)(2,1)} %get-tuple-element.10), channel_id=1, source_target_pairs={{0,1},{1,2},{2,3},{4,5},{5,6},{6,7},{8,9},{9,10},{10,11},{12,13},{... | collective-permute-start | bytes 129032 | tf_op jit(solution)/shard_map/ppermute | solution.py:122
  113.4 1.3 collective-permute-start.7
  115.3 43.4 %psum.21 = bf16[50,512]{1,0:T(8,128)(2,1)} all-reduce(bf16[50,512]{1,0:T(8,128)(2,1)} %pad_maximum_fusion.3), channel_id=1, replica_groups=mesh['rows'=8,'cols'=4] {'rows','cols'}, use_global_device_ids=true, to_apply=%region_5.6 | all-reduce | flops 25600 | bytes 102400 | tf_op jit(solution)/shard_map/psum | solution.py:187
  160.0 1.5 slice.52
  161.5 3.1 %fusion.19.refs_0_ = bf16[14,144,512]{2,1,0:T(8,128)(2,1)} fusion(bf16[14,3,512]{2,1,0:T(4,128)(2,1)} %collective-permute-done.7, bf16[14,3,512]{2,1,0:T(4,128)(2,1)} %collective-permute-done.6, bf16[3,128,512]{2,1,0:T(8,128)(2,1)S(1)} %collective-permute-done.5, bf16[8,128,512]{2,1,0:T(8,128)(2,1)S(1)} %bitcast.32, ...), kind=kLoop, calls=%fused_computation.30 | loop fusion | flops 16515072 | bytes 3985408 | tf_op jit(solution)/shard_map/concatenate | solution.py:126
  164.5 10.8 %conv.3 = bf16[8,128,512]{2,1,0:T(8,128)(2,1)} custom-call(bf16[14,144,512]{2,1,0:T(8,128)(2,1)} %fusion.19.refs_0_, f32[49,512]{1,0:T(8,128)} %rev.3.refs_1_, bf16[8,128,512]{2,1,0:T(8,128)(2,1)} %refs_2_.1), custom_call_target="tpu_custom_call" | custom-call | flops 52428800 | bytes 2097152 | tf_op jit(solution)/shard_map/conv/pallas_call | solution.py:81
  175.3 50.2 %all-reduce.5.cloned.1.call-done = (bf16[512,2048]{1,0:T(8,128)(2,1)}, bf16[2048,512]{1,0:T(8,128)(2,1)}) async-done(((bf16[512,2048]{1,0:T(8,128)(2,1)}, bf16[2048,512]{1,0:T(8,128)(2,1)}), (bf16[512,2048]{1,0:T(8,128)(2,1)}, bf16[2048,512]{1,0:T(8,128)(2,1)})) %all-reduce.5.cloned.1.call-update) | async-done | bytes 4194320 | tf_op jit(solution)/shard_map/psum | solution.py:187
  225.5 4.3 %convert_element_type.36 = f32[512,2048]{1,0:T(8,128)} convert(bf16[512,2048]{1,0:T(8,128)(2,1)} %get-tuple-element.8) | non-fusion elementwise | flops 1048576 | bytes 6291456 | tf_op jit(solution)/shard_map/convert_element_type | solution.py:196
  229.8 2.6 %convert_element_type.39 = f32[2048,512]{1,0:T(8,128)} convert(bf16[2048,512]{1,0:T(8,128)(2,1)S(1)} %copy-done.6) | non-fusion elementwise | flops 1048576 | bytes 6291456 | tf_op jit(solution)/shard_map/convert_element_type | solution.py:197
  (42 shorter events, 5.8 us)
Async XLA Ops:
  7.2 49.0 %copy-start = (bf16[512,2048]{1,0:T(8,128)(2,1)S(1)}, bf16[512,2048]{1,0:T(8,128)(2,1)}, u32[]{:S(2)}) copy-start(bf16[512,2048]{1,0:T(8,128)(2,1)} %param.9) | copy-start | bytes 6291460
  7.2 23.1 %copy-start.5 = (bf16[8,128,512]{2,1,0:T(8,128)(2,1)S(1)}, bf16[8,128,512]{2,1,0:T(8,128)(2,1)}, u32[]{:S(2)}) copy-start(bf16[8,128,512]{2,1,0:T(8,128)(2,1)} %param.6) | copy-start | bytes 3145732
  7.2 218.3 %all-reduce.5.cloned.1.call-start = ((), (), s32[]{:S(2)}) async-start(), calls=%async_computation | async-start | bytes 8388608 | tf_op jit(solution)/shard_map/psum | solution.py:187
  8.6 21.7 %collective-permute-start = (bf16[3,128,512]{2,1,0:T(8,128)(2,1)S(1)}, bf16[3,128,512]{2,1,0:T(8,128)(2,1)S(1)}, u32[]{:S(2)}, u32[]{:S(2)}) collective-permute-start(bf16[3,128,512]{2,1,0:T(8,128)(2,1)S(1)} %get-tuple-element.17), channel_id=1, source_target_pairs={{0,4},{4,8},{8,12},{12,16},{16,20},{20,24},{24,28},{1,5},{5,9},{9,... | collective-permute-start | bytes 1179656 | tf_op jit(solution)/shard_map/ppermute | solution.py:122
  13.5 16.9 %collective-permute-start.1 = (bf16[3,128,512]{2,1,0:T(8,128)(2,1)S(1)}, bf16[3,128,512]{2,1,0:T(8,128)(2,1)S(1)}, u32[]{:S(2)}, u32[]{:S(2)}) collective-permute-start(bf16[3,128,512]{2,1,0:T(8,128)(2,1)S(1)} %get-tuple-element.16), channel_id=1, source_target_pairs={{4,0},{8,4},{12,8},{16,12},{20,16},{24,20},{28,24},{5,1},{9,5},{13... | collective-permute-start | bytes 1179656 | tf_op jit(solution)/shard_map/ppermute | solution.py:125
  30.5 2.6 %collective-permute-start.2 = (bf16[14,3,512]{2,1,0:T(4,128)(2,1)S(1)}, bf16[14,3,512]{2,1,0:T(4,128)(2,1)S(1)}, u32[]{:S(2)}, u32[]{:S(2)}) collective-permute-start(bf16[14,3,512]{2,1,0:T(4,128)(2,1)S(1)} %get-tuple-element.12), channel_id=1, source_target_pairs={{0,1},{1,2},{2,3},{4,5},{5,6},{6,7},{8,9},{9,10},{10,11},{12,13},{... | collective-permute-start | bytes 129032 | tf_op jit(solution)/shard_map/ppermute | solution.py:122
  31.9 4.9 %collective-permute-start.3 = (bf16[14,3,512]{2,1,0:T(4,128)(2,1)S(1)}, bf16[14,3,512]{2,1,0:T(4,128)(2,1)S(1)}, u32[]{:S(2)}, u32[]{:S(2)}) collective-permute-start(bf16[14,3,512]{2,1,0:T(4,128)(2,1)S(1)} %get-tuple-element.13), channel_id=1, source_target_pairs={{1,0},{2,1},{3,2},{5,4},{6,5},{7,6},{9,8},{10,9},{11,10},{13,12},{... | collective-permute-start | bytes 129032 | tf_op jit(solution)/shard_map/ppermute | solution.py:125
  51.7 4.0 %copy-start.8 = (f32[512]{0:T(512)S(1)}, f32[512]{0:T(512)}, u32[]{:S(2)}) copy-start(f32[512]{0:T(512)} %param.8) | copy-start | bytes 6148
  53.6 2.2 copy-start.1
  56.1 2.4 copy-start.7
  58.5 4.0 %copy-start.9 = (bf16[2048,512]{1,0:T(8,128)(2,1)S(1)}, bf16[2048,512]{1,0:T(8,128)(2,1)}, u32[]{:S(2)}) copy-start(bf16[2048,512]{1,0:T(8,128)(2,1)} %param.10) | copy-start | bytes 6291460
  67.5 2.0 copy-start.10
  73.4 5.8 %copy-start.2 = (f32[8,128,512]{2,1,0:T(8,128)S(1)}, f32[8,128,512]{2,1,0:T(8,128)}, u32[]{:S(2)}) copy-start(f32[8,128,512]{2,1,0:T(8,128)} %conv.2) | copy-start | bytes 6291460
  80.2 11.1 %copy-start.3 = (bf16[1024,512]{1,0:T(8,128)(2,1)}, bf16[1024,512]{1,0:T(8,128)(2,1)S(1)}, u32[]{:S(2)}) copy-start(bf16[1024,512]{1,0:T(8,128)(2,1)S(1)} %multiply_convert_fusion.4) | copy-start | bytes 3145732
  81.3 20.3 %collective-permute-start.5 = (bf16[3,128,512]{2,1,0:T(8,128)(2,1)}, bf16[3,128,512]{2,1,0:T(8,128)(2,1)S(1)}, u32[]{:S(2)}, u32[]{:S(2)}) collective-permute-start(bf16[3,128,512]{2,1,0:T(8,128)(2,1)} %bitcast.6), channel_id=1, source_target_pairs={{4,0},{8,4},{12,8},{16,12},{20,16},{24,20},{28,24},{5,1},{9,5},{13... | collective-permute-start | bytes 1179656 | tf_op jit(solution)/shard_map/ppermute | solution.py:125
  82.6 26.1 %collective-permute-start.4 = (bf16[3,128,512]{2,1,0:T(8,128)(2,1)}, bf16[3,128,512]{2,1,0:T(8,128)(2,1)}, u32[]{:S(2)}, u32[]{:S(2)}) collective-permute-start(bf16[3,128,512]{2,1,0:T(8,128)(2,1)} %bitcast.4), channel_id=1, source_target_pairs={{0,4},{4,8},{8,12},{12,16},{16,20},{20,24},{24,28},{1,5},{5,9},{9,... | collective-permute-start | bytes 1179656 | tf_op jit(solution)/shard_map/ppermute | solution.py:122
  100.6 60.8 %copy-start.4 = (bf16[1024,512]{1,0:T(8,128)(2,1)S(1)}, bf16[1024,512]{1,0:T(8,128)(2,1)}, u32[]{:S(2)}) copy-start(bf16[1024,512]{1,0:T(8,128)(2,1)} %copy-done.3) | copy-start | bytes 3145732
  110.3 51.2 %collective-permute-start.6 = (bf16[14,3,512]{2,1,0:T(4,128)(2,1)}, bf16[14,3,512]{2,1,0:T(4,128)(2,1)}, u32[]{:S(2)}, u32[]{:S(2)}) collective-permute-start(bf16[14,3,512]{2,1,0:T(4,128)(2,1)} %get-tuple-element.10), channel_id=1, source_target_pairs={{0,1},{1,2},{2,3},{4,5},{5,6},{6,7},{8,9},{9,10},{10,11},{12,13},{... | collective-permute-start | bytes 129032 | tf_op jit(solution)/shard_map/ppermute | solution.py:122
  113.4 48.1 %collective-permute-start.7 = (bf16[14,3,512]{2,1,0:T(4,128)(2,1)}, bf16[14,3,512]{2,1,0:T(4,128)(2,1)}, u32[]{:S(2)}, u32[]{:S(2)}) collective-permute-start(bf16[14,3,512]{2,1,0:T(4,128)(2,1)} %get-tuple-element.11), channel_id=1, source_target_pairs={{1,0},{2,1},{3,2},{5,4},{6,5},{7,6},{9,8},{10,9},{11,10},{13,12},{... | collective-permute-start | bytes 129032 | tf_op jit(solution)/shard_map/ppermute | solution.py:125
  225.5 4.3 %copy-start.6 = (bf16[2048,512]{1,0:T(8,128)(2,1)S(1)}, bf16[2048,512]{1,0:T(8,128)(2,1)}, u32[]{:S(2)}) copy-start(bf16[2048,512]{1,0:T(8,128)(2,1)} %get-tuple-element.9) | copy-start | bytes 6291460
Sparse Core Ops, SparseCore 0:
  73.5 151.9 all-reduce.4
